TPU v7x, 32 devices: a whole 2x2x4 slice. The times are simulated.
32 devices in a mesh: fsdp: 8 (over z, y), tp: 4 (over x, core).
Axes of the slice: x: 2, y: 2, z: 4, core: 2. Of those that a mesh axis runs over, the one named last changes fastest.
Arguments:
- block_in: bfloat16 [8192, 2048], P(('fsdp', 'tp')), may hold values from -6 to 6
- segment_ids: int32 [8192], P('fsdp'), may hold values from 0 to 31, never falling along the last dimension, each value on 1 to 512 neighbouring positions
- w_query: bfloat16 [2048, 2048], P('fsdp', 'tp'), may hold values from -0.125 to 0.125
- w_key: bfloat16 [2048, 2048], P('fsdp', 'tp'), may hold values from -0.125 to 0.125
- w_value: bfloat16 [2048, 2048], P('fsdp', 'tp'), may hold values from -0.125 to 0.125
- w_out: bfloat16 [2048, 2048], P('fsdp', 'tp'), may hold values from -0.125 to 0.125
- w_gate: bfloat16 [2048, 8192], P('fsdp', 'tp'), may hold values from -0.125 to 0.125
- w_up: bfloat16 [2048, 8192], P('fsdp', 'tp'), may hold values from -0.125 to 0.125
- w_down: bfloat16 [2048, 8192], P('fsdp', 'tp'), may hold values from -0.0625 to 0.0625
- gains: bfloat16 [4, 2048], replicated, may hold values from 0.25 to 1.75
- out_cotangent: bfloat16 [8192, 2048], P(('fsdp', 'tp')), may hold values from -18 to 18
Outputs:
- block_out: bfloat16 [8192, 2048], P(('fsdp', 'tp'))
- input_grad: bfloat16 [8192, 2048], P(('fsdp', 'tp'))
- query_grad: float32 [2048, 2048], P('fsdp', 'tp')
- key_grad: float32 [2048, 2048], P('fsdp', 'tp')
- value_grad: float32 [2048, 2048], P('fsdp', 'tp')
- output_grad: float32 [2048, 2048], P('fsdp', 'tp')
- gate_grad: float32 [2048, 8192], P('fsdp', 'tp')
- up_grad: float32 [2048, 8192], P('fsdp', 'tp')
- down_grad: float32 [2048, 8192], P('fsdp', 'tp')
- gains_grad: float32 [4, 2048], replicated
Inputs may be any that keep to these rules, and one draw needn't show every extreme that they name: `segment_ids`: segment ids never fall along the tokens; a segment covers 1 to 512 consecutive tokens.
All inputs are finite; a program needn't handle non-finite values.
Results may differ from a plain program's by a relative error of at most 0.02.
Values may be sent and summed in bfloat16 or wider, within the bound.
A program may use at most 192 MiB of HBM per device.

v0:
```python
import jax
import jax.numpy as jnp
from jax import lax
from jax.sharding import PartitionSpec as P

HD = 128
LEN = 1024
EPSILON = 1e-06
THETA = 500000.0
NEG_LARGE = -1e30


def dot_plain(left, right):
    return jnp.dot(left, right, preferred_element_type=jnp.float32)


def dot_rows(left, right):
    return lax.dot_general(
        left, right, (((1,), (1,)), ((), ())), preferred_element_type=jnp.float32
    )


def dot_cols(left, right):
    return lax.dot_general(
        left, right, (((0,), (0,)), ((), ())), preferred_element_type=jnp.float32
    )


def rotate_half(values):
    front_half = values[..., : HD // 2]
    back_half = values[..., HD // 2 :]
    return jnp.concatenate([-back_half, front_half], axis=-1)


def rotate_back(values):
    front_half = values[..., : HD // 2]
    back_half = values[..., HD // 2 :]
    return jnp.concatenate([back_half, -front_half], axis=-1)


def rotary(values, cosine, sine):
    return values * cosine + rotate_half(values) * sine


def unrotary(values, cosine, sine):
    return values * cosine + rotate_back(values * sine)


def rope_tables(row_count):
    positions = (jnp.arange(row_count, dtype=jnp.int32) % LEN).astype(jnp.float32)
    freq_index = jnp.arange(HD // 2, dtype=jnp.float32)
    frequency = THETA ** (-2.0 * freq_index / HD)
    angles = positions[:, None] * frequency[None, :]
    angles = jnp.concatenate([angles, angles], axis=1)[:, None, :]
    return (jnp.cos(angles), jnp.sin(angles))


def norm_back(unit_rows, scales, grad_unit):
    return scales * (
        grad_unit - unit_rows * jnp.mean(grad_unit * unit_rows, axis=-1, keepdims=True)
    )


def local(
    block_in,
    segment_ids,
    w_query,
    w_key,
    w_value,
    w_out,
    w_gate,
    w_up,
    w_down,
    gains,
    out_cotangent,
):
    tp_index = lax.axis_index("tp")
    model_width = block_in.shape[1]
    heads_width = w_query.shape[1]
    local_heads = heads_width // HD
    group_rows = segment_ids.shape[0]
    seq_count = group_rows // LEN
    block_rows = min(512, LEN)
    block_count = LEN // block_rows
    scale_factor = HD ** (-0.5)
    gain_values = gains.astype(jnp.float32)
    head_gains = lax.dynamic_slice_in_dim(gain_values, tp_index * heads_width, heads_width, 1)
    cosine, sine = rope_tables(group_rows)
    seq_ids = segment_ids.reshape(seq_count, LEN)
    key_positions = jnp.arange(LEN, dtype=jnp.int32)
    gathered_in = lax.all_gather(block_in, "tp", axis=0, tiled=True)
    weights_fwd = (
        lax.all_gather(w_query, "fsdp", axis=0, tiled=True),
        lax.all_gather(w_key, "fsdp", axis=0, tiled=True),
        lax.all_gather(w_value, "fsdp", axis=0, tiled=True),
        lax.all_gather(w_out, "fsdp", axis=0, tiled=True),
        lax.all_gather(w_gate, "fsdp", axis=0, tiled=True),
        lax.all_gather(w_up, "fsdp", axis=0, tiled=True),
        lax.all_gather(w_down, "fsdp", axis=0, tiled=True),
    )
    query_full, key_full, value_full, out_full, gate_full, up_full, down_full = weights_fwd
    query_raw = dot_plain(gathered_in, query_full)
    key_raw = dot_plain(gathered_in, key_full)
    value_low = dot_plain(gathered_in, value_full).astype(jnp.bfloat16)
    square_sums = lax.psum(
        (jnp.sum(query_raw * query_raw, axis=1), jnp.sum(key_raw * key_raw, axis=1)), "tp"
    )
    query_scale = lax.rsqrt(square_sums[0] / model_width + EPSILON)[:, None]
    key_scale = lax.rsqrt(square_sums[1] / model_width + EPSILON)[:, None]
    query_unit = query_raw * query_scale
    key_unit = key_raw * key_scale
    query_rot = rotary(
        (query_unit * head_gains[0]).reshape(group_rows, local_heads, HD), cosine, sine
    )
    key_rot = rotary((key_unit * head_gains[1]).reshape(group_rows, local_heads, HD), cosine, sine)
    query_seq = query_rot.astype(jnp.bfloat16).reshape(seq_count, LEN, local_heads, HD)
    key_seq = key_rot.astype(jnp.bfloat16).reshape(seq_count, LEN, local_heads, HD)
    value_seq = value_low.reshape(seq_count, LEN, local_heads, HD)

    def block_scores(seq_index, first_row):
        query_block = lax.dynamic_slice_in_dim(query_seq[seq_index], first_row, block_rows, 0)
        ids_row = seq_ids[seq_index]
        query_ids = lax.dynamic_slice_in_dim(ids_row, first_row, block_rows, 0)
        query_positions = first_row + jnp.arange(block_rows, dtype=jnp.int32)
        visible = (query_ids[:, None] == ids_row[None, :]) & (
            key_positions[None, :] <= query_positions[:, None]
        )
        scores = (
            jnp.einsum(
                "qhd,khd->hqk", query_block, key_seq[seq_index], preferred_element_type=jnp.float32
            )
            * scale_factor
        )
        return (jnp.where(visible[None, :, :], scores, NEG_LARGE), query_block)

    def attend_block(flat_index):
        seq_index = flat_index // block_count
        first_row = flat_index % block_count * block_rows
        scores, query_block = block_scores(seq_index, first_row)
        row_max = jnp.max(scores, axis=-1, keepdims=True)
        exponent = jnp.exp(scores - row_max)
        row_total = jnp.sum(exponent, axis=-1, keepdims=True)
        probs_low = (exponent / row_total).astype(jnp.bfloat16)
        context = jnp.einsum(
            "hqk,khd->qhd", probs_low, value_seq[seq_index], preferred_element_type=jnp.float32
        )
        return (context.astype(jnp.bfloat16), (row_max + jnp.log(row_total))[..., 0])

    contexts, log_totals = lax.map(
        attend_block, jnp.arange(seq_count * block_count, dtype=jnp.int32)
    )
    context_low = contexts.reshape(group_rows, heads_width)
    log_totals = log_totals.reshape(seq_count, block_count, local_heads, block_rows)
    attn_terms = dot_rows(context_low, out_full)
    attn_sum = lax.psum_scatter(attn_terms, "tp", scatter_dimension=0, tiled=True)
    attn_scale = lax.rsqrt(jnp.mean(attn_sum * attn_sum, axis=1, keepdims=True) + EPSILON)
    attn_unit = attn_sum * attn_scale
    hidden_mid = block_in.astype(jnp.float32) + attn_unit * gain_values[2]
    hidden_group = lax.all_gather(hidden_mid.astype(jnp.bfloat16), "tp", axis=0, tiled=True)
    gate_raw = dot_plain(hidden_group, gate_full)
    up_raw = dot_plain(hidden_group, up_full)
    sigmoid_gate = jax.nn.sigmoid(gate_raw)
    silu_gate = gate_raw * sigmoid_gate
    inner_low = (silu_gate * up_raw).astype(jnp.bfloat16)
    mlp_terms = dot_rows(inner_low, down_full)
    mlp_sum = lax.psum_scatter(mlp_terms, "tp", scatter_dimension=0, tiled=True)
    mlp_scale = lax.rsqrt(jnp.mean(mlp_sum * mlp_sum, axis=1, keepdims=True) + EPSILON)
    mlp_unit = mlp_sum * mlp_scale
    block_out = (hidden_mid + mlp_unit * gain_values[3]).astype(jnp.bfloat16)
    weights_bwd = (
        lax.all_gather(w_query, "fsdp", axis=0, tiled=True),
        lax.all_gather(w_key, "fsdp", axis=0, tiled=True),
        lax.all_gather(w_value, "fsdp", axis=0, tiled=True),
        lax.all_gather(w_out, "fsdp", axis=0, tiled=True),
        lax.all_gather(w_gate, "fsdp", axis=0, tiled=True),
        lax.all_gather(w_up, "fsdp", axis=0, tiled=True),
        lax.all_gather(w_down, "fsdp", axis=0, tiled=True),
    )
    query_back_w, key_back_w, value_back_w, out_back_w, gate_back_w, up_back_w, down_back_w = (
        weights_bwd
    )
    grad_final = out_cotangent.astype(jnp.float32)
    mlp_gain_term = jnp.sum(grad_final * mlp_unit, axis=0)
    mixed_back = norm_back(mlp_unit, mlp_scale, grad_final * gain_values[3]).astype(jnp.bfloat16)
    mixed_group = lax.all_gather(mixed_back, "tp", axis=0, tiled=True)
    inner_back = dot_plain(mixed_group, down_back_w)
    down_grad = dot_cols(mixed_group, inner_low)
    gate_back = (
        inner_back * up_raw * sigmoid_gate * (1.0 + gate_raw * (1.0 - sigmoid_gate))
    ).astype(jnp.bfloat16)
    up_back = (inner_back * silu_gate).astype(jnp.bfloat16)
    gate_grad = dot_cols(hidden_group, gate_back)
    up_grad = dot_cols(hidden_group, up_back)
    hidden_terms = dot_rows(gate_back, gate_back_w) + dot_rows(up_back, up_back_w)
    hidden_back = grad_final + lax.psum_scatter(hidden_terms, "tp", scatter_dimension=0, tiled=True)
    attn_gain_term = jnp.sum(hidden_back * attn_unit, axis=0)
    attention_back = norm_back(attn_unit, attn_scale, hidden_back * gain_values[2]).astype(
        jnp.bfloat16
    )
    attention_group = lax.all_gather(attention_back, "tp", axis=0, tiled=True)
    context_back = dot_plain(attention_group, out_back_w).astype(jnp.bfloat16)
    output_grad = dot_cols(attention_group, context_low)
    context_back_seq = context_back.reshape(seq_count, LEN, local_heads, HD)

    def sequence_back(seq_index):
        seq_values = value_seq[seq_index]
        seq_keys = key_seq[seq_index]

        def block_back(accum_pair, block_index):
            keys_back, values_back = accum_pair
            first_row = block_index * block_rows
            scores, query_block = block_scores(seq_index, first_row)
            prob_values = jnp.exp(scores - log_totals[seq_index, block_index][..., None])
            probs_low = prob_values.astype(jnp.bfloat16)
            grad_block = lax.dynamic_slice_in_dim(
                context_back_seq[seq_index], first_row, block_rows, 0
            )
            probs_back = jnp.einsum(
                "qhd,khd->hqk", grad_block, seq_values, preferred_element_type=jnp.float32
            )
            row_delta = jnp.sum(prob_values * probs_back, axis=-1, keepdims=True)
            scores_back = (prob_values * (probs_back - row_delta)).astype(jnp.bfloat16)
            query_part = (
                jnp.einsum(
                    "hqk,khd->qhd", scores_back, seq_keys, preferred_element_type=jnp.float32
                )
                * scale_factor
            )
            keys_back = (
                keys_back
                + jnp.einsum(
                    "hqk,qhd->khd", scores_back, query_block, preferred_element_type=jnp.float32
                )
                * scale_factor
            )
            values_back = values_back + jnp.einsum(
                "hqk,qhd->khd", probs_low, grad_block, preferred_element_type=jnp.float32
            )
            return ((keys_back, values_back), query_part)

        zeros_seq = jnp.zeros((LEN, local_heads, HD), jnp.float32)
        (keys_back, values_back), query_parts = lax.scan(
            block_back, (zeros_seq, zeros_seq), jnp.arange(block_count, dtype=jnp.int32)
        )
        return (query_parts.reshape(LEN, local_heads, HD), keys_back, values_back)

    rot_query_back, rot_key_back, value_parts = lax.map(
        sequence_back, jnp.arange(seq_count, dtype=jnp.int32)
    )
    query_norm_back = unrotary(rot_query_back.reshape(group_rows, local_heads, HD), cosine, sine)
    query_norm_back = query_norm_back.reshape(group_rows, heads_width)
    key_norm_back = unrotary(rot_key_back.reshape(group_rows, local_heads, HD), cosine, sine)
    key_norm_back = key_norm_back.reshape(group_rows, heads_width)
    value_back = value_parts.reshape(group_rows, heads_width).astype(jnp.bfloat16)
    query_gain_term = jnp.sum(query_norm_back * query_unit, axis=0)
    key_gain_term = jnp.sum(key_norm_back * key_unit, axis=0)
    query_unit_back = query_norm_back * head_gains[0]
    key_unit_back = key_norm_back * head_gains[1]
    dot_sums = lax.psum(
        (jnp.sum(query_unit_back * query_unit, axis=1), jnp.sum(key_unit_back * key_unit, axis=1)),
        "tp",
    )
    query_back = (
        query_scale * (query_unit_back - query_unit * (dot_sums[0] / model_width)[:, None])
    ).astype(jnp.bfloat16)
    key_back = (
        key_scale * (key_unit_back - key_unit * (dot_sums[1] / model_width)[:, None])
    ).astype(jnp.bfloat16)
    input_terms = (
        dot_rows(query_back, query_back_w)
        + dot_rows(key_back, key_back_w)
        + dot_rows(value_back, value_back_w)
    )
    input_back = lax.psum_scatter(
        input_terms.astype(jnp.bfloat16), "tp", scatter_dimension=0, tiled=True
    ).astype(jnp.float32)
    input_grad = (hidden_back + input_back).astype(jnp.bfloat16)
    query_grad = dot_cols(gathered_in, query_back)
    key_grad = dot_cols(gathered_in, key_back)
    value_grad = dot_cols(gathered_in, value_back)
    weight_sums = (
        lax.psum_scatter(
            query_grad.astype(jnp.bfloat16), "fsdp", scatter_dimension=0, tiled=True
        ).astype(jnp.float32),
        lax.psum_scatter(
            key_grad.astype(jnp.bfloat16), "fsdp", scatter_dimension=0, tiled=True
        ).astype(jnp.float32),
        lax.psum_scatter(
            value_grad.astype(jnp.bfloat16), "fsdp", scatter_dimension=0, tiled=True
        ).astype(jnp.float32),
        lax.psum_scatter(
            output_grad.astype(jnp.bfloat16), "fsdp", scatter_dimension=0, tiled=True
        ).astype(jnp.float32),
        lax.psum_scatter(
            gate_grad.astype(jnp.bfloat16), "fsdp", scatter_dimension=0, tiled=True
        ).astype(jnp.float32),
        lax.psum_scatter(
            up_grad.astype(jnp.bfloat16), "fsdp", scatter_dimension=0, tiled=True
        ).astype(jnp.float32),
        lax.psum_scatter(
            down_grad.astype(jnp.bfloat16), "fsdp", scatter_dimension=0, tiled=True
        ).astype(jnp.float32),
    )
    head_terms = jnp.stack([query_gain_term, key_gain_term])
    placed = lax.dynamic_update_slice(
        jnp.zeros((2, model_width), jnp.float32), head_terms, (jnp.int32(0), tp_index * heads_width)
    )
    gain_terms = jnp.concatenate([placed, jnp.stack([attn_gain_term, mlp_gain_term])], axis=0)
    gains_grad = lax.psum(gain_terms, ("fsdp", "tp"))
    return (
        block_out,
        input_grad,
        weight_sums[0],
        weight_sums[1],
        weight_sums[2],
        weight_sums[3],
        weight_sums[4],
        weight_sums[5],
        weight_sums[6],
        gains_grad,
    )


def solution(mesh):
    in_specs = (
        P(("fsdp", "tp"), None),
        P("fsdp"),
        P("fsdp", "tp"),
        P("fsdp", "tp"),
        P("fsdp", "tp"),
        P("fsdp", "tp"),
        P("fsdp", "tp"),
        P("fsdp", "tp"),
        P("fsdp", "tp"),
        P(),
        P(("fsdp", "tp"), None),
    )
    out_specs = (
        P(("fsdp", "tp"), None),
        P(("fsdp", "tp"), None),
        P("fsdp", "tp"),
        P("fsdp", "tp"),
        P("fsdp", "tp"),
        P("fsdp", "tp"),
        P("fsdp", "tp"),
        P("fsdp", "tp"),
        P("fsdp", "tp"),
        P(),
    )
    return jax.shard_map(local, mesh=mesh, in_specs=in_specs, out_specs=out_specs, check_vma=False)
```

profile of v0, /device:TPU:0, one launch (start us, length us, event | category | flops | bytes accessed | tf_op | source)
XLA Modules:
  0.0 1814.4 jit_solution(8109534931990387546)
XLA Ops:
  13.2 48.7 %all-gather.14.cloned.1.call-done = bf16[2048,512]{1,0:T(8,128)(2,1)} async-done(((bf16[256,512]{1,0:T(8,128)(2,1)}), bf16[2048,512]{1,0:T(8,128)(2,1)}) %all-gather.14.cloned.1.call-update) | async-done | bytes 2097168 | tf_op jit(solution)/shard_map/all_gather | solution.py:93
  62.0 34.6 %all-gather.12.cloned.1.call-done = bf16[1024,2048]{1,0:T(8,128)(2,1)} async-done(((bf16[256,2048]{1,0:T(8,128)(2,1)}), bf16[1024,2048]{1,0:T(8,128)(2,1)}) %all-gather.12.cloned.1.call-update) | async-done | bytes 4194320 | tf_op jit(solution)/shard_map/all_gather | solution.py:91
  96.5 6.6 multiply_reduce_fusion.9
  103.1 44.7 %all-gather.16.cloned.1.call-done = bf16[2048,512]{1,0:T(8,128)(2,1)} async-done(((bf16[256,512]{1,0:T(8,128)(2,1)}), bf16[2048,512]{1,0:T(8,128)(2,1)}) %all-gather.16.cloned.1.call-update) | async-done | bytes 2097168 | tf_op jit(solution)/shard_map/all_gather | solution.py:94
  147.8 5.3 multiply_reduce_fusion.8
  153.1 6.0 all-reduce.1
  180.3 17.1 all-gather.18.cloned.1.call-done
  197.4 5.2 convolution_convert_fusion.8
  204.1 6.1 fusion.60
  210.2 23.4 %while.42 = (s32[]{:T(128)}, bf16[2,512,4,128]{3,2,1,0:T(4,128)(2,1)}, f32[2,4,512]{2,1,0:T(4,128)S(1)}, s32[2]{0:T(128)S(1)}, s32[1,1024]{1,0:T(1,128)S(1)}, /*...) while((s32[]{:T(128)}, ...), condition=%wide.region_7.8_spmd.clone, body=%wide.region_4.7_spmd.clone.sunk | while | flops 1100741120 | bytes 35732304 | solution.py:149
  233.6 13.4 all-gather.20.cloned.1.call-done
  247.0 7.6 fusion.66
  255.5 69.3 %reduce-scatter.12.cloned.1.call-done = f32[256,2048]{1,0:T(8,128)} async-done(((f32[1024,2048]{1,0:T(8,128)}), f32[256,2048]{1,0:T(8,128)}) %reduce-scatter.12.cloned.1.call-update) | async-done | bytes 2097168 | tf_op jit(solution)/shard_map/reduce_scatter | solution.py:155
  329.8 121.7 %all-gather.24.cloned.1.call-done = bf16[2048,2048]{1,0:T(8,128)(2,1)} async-done(((bf16[256,2048]{1,0:T(8,128)(2,1)}), bf16[2048,2048]{1,0:T(8,128)(2,1)}) %all-gather.24.cloned.1.call-update) | async-done | bytes 8388624 | tf_op jit(solution)/shard_map/all_gather | solution.py:97
  451.4 34.8 %all-gather.22.cloned.1.call-done = bf16[1024,2048]{1,0:T(8,128)(2,1)} async-done(((bf16[256,2048]{1,0:T(8,128)(2,1)}), bf16[1024,2048]{1,0:T(8,128)(2,1)}) %all-gather.22.cloned.1.call-update) | async-done | bytes 4194320 | tf_op jit(solution)/shard_map/all_gather | solution.py:159
  486.2 15.0 fusion.81
  501.2 111.7 %all-gather.26.cloned.1.call-done = bf16[2048,2048]{1,0:T(8,128)(2,1)} async-done(((bf16[256,2048]{1,0:T(8,128)(2,1)}), bf16[2048,2048]{1,0:T(8,128)(2,1)}) %all-gather.26.cloned.1.call-update) | async-done | bytes 8388624 | tf_op jit(solution)/shard_map/all_gather | solution.py:98
  612.9 17.0 multiply_convert_fusion.3
  629.9 107.7 %all-gather.28.cloned.1.call-done = bf16[2048,2048]{1,0:T(8,128)(2,1)} async-done(((bf16[256,2048]{1,0:T(8,128)(2,1)}), bf16[2048,2048]{1,0:T(8,128)(2,1)}) %all-gather.28.cloned.1.call-update) | async-done | bytes 8388624 | tf_op jit(solution)/shard_map/all_gather | solution.py:99
  737.6 14.6 fusion.82
  752.3 69.7 %reduce-scatter.14.cloned.1.call-done = f32[256,2048]{1,0:T(8,128)} async-done(((f32[1024,2048]{1,0:T(8,128)}), f32[256,2048]{1,0:T(8,128)}) %reduce-scatter.14.cloned.1.call-update) | async-done | bytes 2097168 | tf_op jit(solution)/shard_map/reduce_scatter | solution.py:166
  827.1 34.6 %all-gather.30.cloned.1.call-done = bf16[1024,2048]{1,0:T(8,128)(2,1)} async-done(((bf16[256,2048]{1,0:T(8,128)(2,1)}), bf16[1024,2048]{1,0:T(8,128)(2,1)}) %all-gather.30.cloned.1.call-update) | async-done | bytes 4194320 | tf_op jit(solution)/shard_map/all_gather | solution.py:185
  861.6 19.9 %multiply_convert_fusion.1 = (bf16[1024,2048]{1,0:T(8,128)(2,1)S(1)}, bf16[1024,2048]{1,0:T(8,128)(2,1)}) fusion(f32[1024,2048]{1,0:T(8,128)} %fusion.81, f32[1024,2048]{1,0:T(8,128)} %get-tuple-element.465, bf16[1024,2048]{1,0:T(8,128)(2,1)} %all-gather.30.cloned.1.call-done, bf16[2048,2048]{1,0:T(8,128)(2,1)} %all-gather.28.cloned.1.call-done), kind=kOutput, calls=%fused_computation.61 | convolution fusion | flops 8617197568 | bytes 37748736 | tf_op jit(solution)/shard_map/dot_general | solution.py:14
  881.5 14.0 fusion.83
  895.6 13.6 convolution_add_fusion
  909.5 71.3 %reduce-scatter.16.cloned.1.call-done = f32[256,2048]{1,0:T(8,128)} async-done(((f32[1024,2048]{1,0:T(8,128)}), f32[256,2048]{1,0:T(8,128)}) %reduce-scatter.16.cloned.1.call-update) | async-done | bytes 2097168 | tf_op jit(solution)/shard_map/reduce_scatter | solution.py:195
  986.4 14.1 convolution_convert_fusion
  1000.5 14.0 convolution_convert_fusion.2
  1015.1 14.1 convolution_convert_fusion.1
  1038.2 6.3 convolution_convert_fusion.7
  1044.5 68.7 %while.43 = (s32[]{:T(128)}, f32[1024,4,128]{0,2,1:T(8,128)S(1)}, f32[1024,4,128]{0,2,1:T(8,128)}, f32[2,512,4,128]{3,1,2,0:T(8,128)}, s32[2]{0:T(128)S(1)}, /*i...) while((s32[]{:T(128)}, f32[1024,4,128]{0,2,1:T(8,128)S(1)}, ...), condition=%wide.region_17.18_spmd.clone, body=%wide.region_15.17_spmd.clone.sunk | while | flops 2720266752 | bytes 163650544 | solution.py:242
  1047.3 5.6 fusion.161
  1054.9 7.6 multiply_reduce_fusion.11
  1081.1 5.6 fusion.161
  1088.6 7.6 multiply_reduce_fusion.11
  1108.1 5.1 bitcast_add_fusion.7
  1141.2 6.7 all-reduce
  1162.4 6.2 convolution_convert_fusion.3
  1170.5 5.9 fusion.50
  1183.1 6.1 add_convert_fusion
  1192.0 130.0 %reduce-scatter.28.cloned.1.call-done = bf16[256,2048]{1,0:T(8,128)(2,1)} async-done(((bf16[2048,2048]{1,0:T(8,128)(2,1)}), bf16[256,2048]{1,0:T(8,128)(2,1)}) %reduce-scatter.28.cloned.1.call-update) | async-done | bytes 1048592 | tf_op jit(solution)/shard_map/reduce_scatter | solution.py:294
  1324.8 147.3 %reduce-scatter.30.cloned.1.call-done = bf16[256,2048]{1,0:T(8,128)(2,1)} async-done(((bf16[2048,2048]{1,0:T(8,128)(2,1)}), bf16[256,2048]{1,0:T(8,128)(2,1)}) %reduce-scatter.30.cloned.1.call-update) | async-done | bytes 1048592 | tf_op jit(solution)/shard_map/reduce_scatter | solution.py:297
  1475.0 40.9 %psum.39 = f32[4,2048]{1,0:T(4,128)} all-reduce(f32[4,2048]{1,0:T(4,128)S(1)} %pad_maximum_fusion.2), channel_id=1, replica_groups=mesh['fsdp'=8,'tp'=4] {'fsdp','tp'}, use_global_device_ids=true, to_apply=%region_34.35 | all-reduce | flops 8192 | bytes 65536 | tf_op jit(solution)/shard_map/psum | solution.py:309
  1515.9 28.3 %reduce-scatter.22.cloned.1.call-done = bf16[256,512]{0,1:T(8,128)(2,1)} async-done(((bf16[2048,512]{0,1:T(8,128)(2,1)}), bf16[256,512]{0,1:T(8,128)(2,1)}) %reduce-scatter.22.cloned.1.call-update) | async-done | bytes 262160 | tf_op jit(solution)/shard_map/reduce_scatter | solution.py:285
  1546.1 69.6 %reduce-scatter.20.cloned.1.call-done = bf16[256,512]{0,1:T(8,128)(2,1)} async-done(((bf16[2048,512]{0,1:T(8,128)(2,1)}), bf16[256,512]{0,1:T(8,128)(2,1)}) %reduce-scatter.20.cloned.1.call-update) | async-done | bytes 262160 | tf_op jit(solution)/shard_map/reduce_scatter | solution.py:282
  1617.6 69.0 %reduce-scatter.26.cloned.1.call-done = bf16[256,512]{1,0:T(8,128)(2,1)} async-done(((bf16[2048,512]{1,0:T(8,128)(2,1)}), bf16[256,512]{1,0:T(8,128)(2,1)}) %reduce-scatter.26.cloned.1.call-update) | async-done | bytes 262160 | tf_op jit(solution)/shard_map/reduce_scatter | solution.py:291
  1688.4 69.9 %reduce-scatter.24.cloned.1.call-done = bf16[256,512]{0,1:T(8,128)(2,1)} async-done(((bf16[2048,512]{0,1:T(8,128)(2,1)}), bf16[256,512]{0,1:T(8,128)(2,1)}) %reduce-scatter.24.cloned.1.call-update) | async-done | bytes 262160 | tf_op jit(solution)/shard_map/reduce_scatter | solution.py:288
  1760.1 44.3 %reduce-scatter.18.cloned.1.call-done = bf16[256,2048]{1,0:T(8,128)(2,1)} async-done(((bf16[1024,2048]{1,0:T(8,128)(2,1)}), bf16[256,2048]{1,0:T(8,128)(2,1)}) %reduce-scatter.18.cloned.1.call-update) | async-done | bytes 1048592 | tf_op jit(solution)/shard_map/reduce_scatter | solution.py:274
  (291 shorter events, 175.1 us)
Async XLA Ops:
  7.2 54.8 %all-gather.14.cloned.1.call-start = ((), (), s32[]{:S(2)}) async-start(), calls=%async_computation.12 | async-start | bytes 2359296 | tf_op jit(solution)/shard_map/all_gather | solution.py:93
  7.9 88.6 %all-gather.12.cloned.1.call-start = ((), (), s32[]{:S(2)}) async-start(), calls=%async_computation.11 | async-start | bytes 5242880 | tf_op jit(solution)/shard_map/all_gather | solution.py:91
  8.7 139.1 %all-gather.16.cloned.1.call-start = ((), (), s32[]{:S(2)}) async-start(), calls=%async_computation.13 | async-start | bytes 2359296 | tf_op jit(solution)/shard_map/all_gather | solution.py:94
  9.4 188.0 %all-gather.18.cloned.1.call-start = ((), (), s32[]{:S(2)}) async-start(), calls=%async_computation.14 | async-start | bytes 2359296 | tf_op jit(solution)/shard_map/all_gather | solution.py:95
  10.0 237.1 %all-gather.20.cloned.1.call-start = ((), (), s32[]{:S(2)}) async-start(), calls=%async_computation.15 | async-start | bytes 2359296 | tf_op jit(solution)/shard_map/all_gather | solution.py:96
  10.6 314.2 %reduce-scatter.12.cloned.1.call-start = ((), (), s32[]{:S(2)}) async-start(), calls=%async_computation.16 | async-start | bytes 10485760 | tf_op jit(solution)/shard_map/reduce_scatter | solution.py:155
  10.8 148.3 %copy-start.47 = (f32[1,512]{1,0:T(1,128)}, f32[1,512]{1,0:T(1,128)S(1)}, u32[]{:S(2)}) copy-start(f32[1,512]{1,0:T(1,128)S(1)} %dynamic-slice.16) | copy-start | bytes 6148
  10.8 155.9 %copy-start.49 = (f32[1,512]{1,0:T(1,128)}, f32[1,512]{1,0:T(1,128)S(1)}, u32[]{:S(2)}) copy-start(f32[1,512]{1,0:T(1,128)S(1)} %constant_dynamic-slice_fusion.2) | copy-start | bytes 6148
  13.2 190.8 %copy-start.23 = (f32[1024,128]{1,0:T(8,128)}, f32[1024,128]{1,0:T(8,128)S(1)}, u32[]{:S(2)}) copy-start(f32[1024,128]{1,0:T(8,128)S(1)} %get-tuple-element.456) | copy-start | bytes 1572868
  13.2 190.8 %copy-start.28 = (f32[1024,128]{1,0:T(8,128)}, f32[1024,128]{1,0:T(8,128)S(1)}, u32[]{:S(2)}) copy-start(f32[1024,128]{1,0:T(8,128)S(1)} %get-tuple-element.457) | copy-start | bytes 1572868
  153.0 7.6 copy-start.16
  159.1 7.6 copy-start.43
  233.6 21.0 %copy-start.2 = (bf16[1,1024,4,128]{3,1,2,0:T(8,128)(2,1)}, bf16[1,1024,4,128]{3,1,2,0:T(8,128)(2,1)S(1)}, u32[]{:S(2)}) copy-start(bf16[1,1024,4,128]{3,1,2,0:T(8,128)(2,1)S(1)} %get-tuple-element.710) | copy-start | bytes 3145732
  233.6 21.0 %copy-start.6 = (bf16[1,1024,4,128]{3,1,2,0:T(8,128)(2,1)}, bf16[1,1024,4,128]{3,1,2,0:T(8,128)(2,1)S(1)}, u32[]{:S(2)}) copy-start(bf16[1,1024,4,128]{3,1,2,0:T(8,128)(2,1)S(1)} %get-tuple-element.711) | copy-start | bytes 3145732
  233.6 21.0 %copy-start.40 = (f32[2,4,512]{2,1,0:T(4,128)}, f32[2,4,512]{2,1,0:T(4,128)S(1)}, u32[]{:S(2)}) copy-start(f32[2,4,512]{2,1,0:T(4,128)S(1)} %get-tuple-element.258) | copy-start | bytes 49156
  254.7 72.1 %copy-start.26 = (bf16[256,2048]{1,0:T(8,128)(2,1)S(1)}, bf16[256,2048]{1,0:T(8,128)(2,1)}, u32[]{:S(2)}) copy-start(bf16[256,2048]{1,0:T(8,128)(2,1)} %param.15) | copy-start | bytes 3145732
  254.7 196.8 %all-gather.24.cloned.1.call-start = ((), (), s32[]{:S(2)}) async-start(), calls=%async_computation.18 | async-start | bytes 9437184 | tf_op jit(solution)/shard_map/all_gather | solution.py:97
  255.4 230.8 %all-gather.22.cloned.1.call-start = ((), (), s32[]{:S(2)}) async-start(), calls=%async_computation.17 | async-start | bytes 5242880 | tf_op jit(solution)/shard_map/all_gather | solution.py:159
  328.4 284.5 %all-gather.26.cloned.1.call-start = ((), (), s32[]{:S(2)}) async-start(), calls=%async_computation.19 | async-start | bytes 9437184 | tf_op jit(solution)/shard_map/all_gather | solution.py:98
  329.1 408.4 %all-gather.28.cloned.1.call-start = ((), (), s32[]{:S(2)}) async-start(), calls=%async_computation.20 | async-start | bytes 9437184 | tf_op jit(solution)/shard_map/all_gather | solution.py:99
  329.7 492.2 %reduce-scatter.14.cloned.1.call-start = ((), (), s32[]{:S(2)}) async-start(), calls=%async_computation.21 | async-start | bytes 10485760 | tf_op jit(solution)/shard_map/reduce_scatter | solution.py:166
  752.2 71.7 %copy-start.11 = (bf16[256,2048]{1,0:T(8,128)(2,1)S(1)}, bf16[256,2048]{1,0:T(8,128)(2,1)}, u32[]{:S(2)}) copy-start(bf16[256,2048]{1,0:T(8,128)(2,1)} %param.25) | copy-start | bytes 3145732
  752.2 109.4 %all-gather.30.cloned.1.call-start = ((), (), s32[]{:S(2)}) async-start(), calls=%async_computation.22 | async-start | bytes 5242880 | tf_op jit(solution)/shard_map/all_gather | solution.py:185
  827.0 153.8 %reduce-scatter.16.cloned.1.call-start = ((), (), s32[]{:S(2)}) async-start(), calls=%async_computation.23 | async-start | bytes 10485760 | tf_op jit(solution)/shard_map/reduce_scatter | solution.py:195
  881.5 14.1 copy-start.56
  909.2 128.9 %all-gather.32.cloned.1.call-start = ((), (), s32[]{:S(2)}) async-start(), calls=%async_computation.24 | async-start | bytes 5242880 | tf_op jit(solution)/shard_map/all_gather | solution.py:200
  986.4 202.9 %reduce-scatter.32.cloned.1.call-start = ((), (), s32[]{:S(2)}) async-start(), calls=%async_computation.32 | async-start | bytes 9437184 | tf_op jit(solution)/shard_map/reduce_scatter | solution.py:300
  1000.5 321.5 %reduce-scatter.28.cloned.1.call-start = ((), (), s32[]{:S(2)}) async-start(), calls=%async_computation.30 | async-start | bytes 9437184 | tf_op jit(solution)/shard_map/reduce_scatter | solution.py:294
  1014.6 457.5 %reduce-scatter.30.cloned.1.call-start = ((), (), s32[]{:S(2)}) async-start(), calls=%async_computation.31 | async-start | bytes 9437184 | tf_op jit(solution)/shard_map/reduce_scatter | solution.py:297
  1029.2 515.0 %reduce-scatter.22.cloned.1.call-start = ((), (), s32[]{:S(2)}) async-start(), calls=%async_computation.27 | async-start | bytes 2359296 | tf_op jit(solution)/shard_map/reduce_scatter | solution.py:285
  1038.1 6.4 copy-start.39
  1038.1 6.4 copy-start.41
  1054.9 7.6 slice-start
  1054.9 7.6 slice-start.1
  1054.9 7.6 copy-start.4
  1066.2 8.4 copy-start
  1088.6 7.6 slice-start
  1088.6 7.6 slice-start.1
  1088.6 7.6 copy-start.4
  1099.9 8.2 copy-start
  1155.1 460.5 %reduce-scatter.20.cloned.1.call-start = ((), (), s32[]{:S(2)}) async-start(), calls=%async_computation.26 | async-start | bytes 2359296 | tf_op jit(solution)/shard_map/reduce_scatter | solution.py:282
  1162.1 524.5 %reduce-scatter.26.cloned.1.call-start = ((), (), s32[]{:S(2)}) async-start(), calls=%async_computation.29 | async-start | bytes 2359296 | tf_op jit(solution)/shard_map/reduce_scatter | solution.py:291
  1168.7 589.6 %reduce-scatter.24.cloned.1.call-start = ((), (), s32[]{:S(2)}) async-start(), calls=%async_computation.28 | async-start | bytes 2359296 | tf_op jit(solution)/shard_map/reduce_scatter | solution.py:288
  1176.4 628.0 %reduce-scatter.18.cloned.1.call-start = ((), (), s32[]{:S(2)}) async-start(), calls=%async_computation.25 | async-start | bytes 5242880 | tf_op jit(solution)/shard_map/reduce_scatter | solution.py:274
  1324.8 150.1 %copy-start.51 = (f32[2048]{0:T(1024)S(1)}, f32[2048]{0:T(1024)}, u32[]{:S(2)}) copy-start(f32[2048]{0:T(1024)} %get-tuple-element.387) | copy-start | bytes 24580
  1324.8 150.1 %copy-start.52 = (f32[2048]{0:T(1024)S(1)}, f32[2048]{0:T(1024)}, u32[]{:S(2)}) copy-start(f32[2048]{0:T(1024)} %get-tuple-element.381) | copy-start | bytes 24580
  1474.9 329.6 %copy-start.12 = (bf16[256,2048]{1,0:T(8,128)(2,1)S(1)}, bf16[256,2048]{1,0:T(8,128)(2,1)}, u32[]{:S(2)}) copy-start(bf16[256,2048]{1,0:T(8,128)(2,1)} %param.25) | copy-start | bytes 3145732
  1474.9 329.6 %copy-start.20 = (f32[256,2048]{1,0:T(8,128)S(1)}, f32[256,2048]{1,0:T(8,128)}, u32[]{:S(2)}) copy-start(f32[256,2048]{1,0:T(8,128)} %reduce-scatter.16.cloned.1.call-done) | copy-start | bytes 6291460
  (41 other events, 132.6 us)
Sparse Core Ops, SparseCore 0:
  10.1 51.7 all-gather.13
  63.5 32.9 all-gather.11
  98.7 49.0 all-gather.15
  149.8 47.6 all-gather.17
  199.4 47.5 all-gather.19
  254.8 69.9 reduce-scatter.11
  326.9 124.4 all-gather.23
  453.6 32.6 all-gather.21
  488.4 124.4 all-gather.25
  614.9 122.6 all-gather.27
  752.3 69.5 reduce-scatter.13
  827.2 34.4 all-gather.29
  909.3 71.4 reduce-scatter.15
  986.5 34.4 all-gather.31
  1024.4 147.4 reduce-scatter.31
  1175.4 146.5 reduce-scatter.27
  1325.5 146.5 reduce-scatter.29
  1475.5 68.6 reduce-scatter.21
  1547.7 67.9 reduce-scatter.19
  1619.1 67.5 reduce-scatter.25
  1690.1 68.0 reduce-scatter.23
  1760.8 43.6 reduce-scatter.17
where the time goes:
time: 1820 us; the launch traced here: 1810 us
  waiting for transfers between devices  1340 us (74%)
  matrix products  261 us (14%)
  other arithmetic  78.8 us (4%)
  blocking collectives  53.6 us (3%)
  local copies, waits for them, and re-layouts  51.2 us (3%)
    reduce_scatter x1, waiting for transfers between devices, local(): lax.psum_scatter(up_grad.astype(jnp.bfloat16), 'fsdp', scatter_dimension=...  147 us
    reduce_scatter x1, waiting for transfers between devices, local(): lax.psum_scatter(gate_grad.astype(jnp.bfloat16), 'fsdp', scatter_dimensio...  130 us
    all_gather x1, waiting for transfers between devices, local(): lax.all_gather(w_gate, 'fsdp', axis=0, tiled=True)  122 us
    all_gather x1, waiting for transfers between devices, local(): lax.all_gather(w_up, 'fsdp', axis=0, tiled=True)  112 us
    all_gather x1, waiting for transfers between devices, local(): lax.all_gather(w_down, 'fsdp', axis=0, tiled=True)  108 us
    dot_general x7, matrix products, dot_plain(): return jnp.dot(left, right, preferred_element_type=jnp.float32)  75.3 us
    reduce_scatter x1, waiting for transfers between devices, local(): lax.psum_scatter(hidden_terms, 'tp', scatter_dimension=0, tiled=True)  71.3 us
    reduce_scatter x1, waiting for transfers between devices, local(): lax.psum_scatter(value_grad.astype(jnp.bfloat16), 'fsdp', scatter_dimensi...  69.9 us
  transfers between devices with their start and end apart: 22, of which 20 were waited for; matrix products, arithmetic and copies ran while one was open for 17% of the time, Pallas kernels for 0%

commit v1 on v0

--- a/solution.py
+++ b/solution.py
@@ -8,6 +8,22 @@
 EPSILON = 1e-06
 THETA = 500000.0
 NEG_LARGE = -1e30
+
+
+def gather_around(x, axis, dim):
+    ways, here, hop = (lax.axis_size(axis), lax.axis_index(axis), x.shape[dim])
+    shape = [n * ways if d == dim else n for d, n in enumerate(x.shape)]
+    full = lax.dynamic_update_slice_in_dim(jnp.zeros(shape, x.dtype), x, here * hop, axis=dim)
+    going_up = going_down = x
+    for far in range(1, ways // 2 + 1):
+        going_up = lax.ppermute(going_up, axis, [(d, (d + 1) % ways) for d in range(ways)])
+        full = lax.dynamic_update_slice_in_dim(full, going_up, (here - far) % ways * hop, axis=dim)
+        if 2 * far < ways:
+            going_down = lax.ppermute(going_down, axis, [(d, (d - 1) % ways) for d in range(ways)])
+            full = lax.dynamic_update_slice_in_dim(
+                full, going_down, (here + far) % ways * hop, axis=dim
+            )
+    return full
 
 
 def dot_plain(left, right):
@@ -95,7 +111,7 @@
         lax.all_gather(w_value, "fsdp", axis=0, tiled=True),
         lax.all_gather(w_out, "fsdp", axis=0, tiled=True),
         lax.all_gather(w_gate, "fsdp", axis=0, tiled=True),
-        lax.all_gather(w_up, "fsdp", axis=0, tiled=True),
+        gather_around(w_up, "fsdp", 0),
         lax.all_gather(w_down, "fsdp", axis=0, tiled=True),
     )
     query_full, key_full, value_full, out_full, gate_full, up_full, down_full = weights_fwd

time: 1820 us -> 1900 us (1.044)
  waiting for transfers between devices: 1340 us -> 1380 us
  starting transfers between devices: 1.75 us -> 31.8 us
  local copies, waits for them, and re-layouts: 51.2 us -> 72.2 us
    ppermute x0 -> x7, waiting for transfers between devices: none -> 191 us  [the longest x4 189 us: gather_around(): lax.ppermute(going_up, axis, [(d, (d + 1) % ways) for d in range(ways)])]
    all_gather x1, waiting for transfers between devices: 122 us -> 0.01 us  [local(): lax.all_gather(w_gate, 'fsdp', axis=0, tiled=True)]
    ppermute x0 -> x7, starting transfers between devices: none -> 30 us  [the longest x3 21.1 us: gather_around(): lax.ppermute(going_down, axis, [(d, (d - 1) % ways) for d in range(ways)])]
    all_gather x1, waiting for transfers between devices: 112 us -> 91.5 us  [local(): lax.all_gather(w_up, 'fsdp', axis=0, tiled=True)]
  transfers between devices with their start and end apart: 22 -> 29, of which waited for: 20 -> 24; matrix products, arithmetic and copies ran while one was open for 17% -> 18% of each run, Pallas kernels for 0% -> 0%
where the time goes in v1:
time: 1900 us
  waiting for transfers between devices  1380 us (73%)
  matrix products  258 us (14%)
  other arithmetic  78.7 us (4%)
  local copies, waits for them, and re-layouts  72.2 us (4%)
  blocking collectives  53.4 us (3%)
  starting transfers between devices  31.8 us (2%)
    ppermute x4, waiting for transfers between devices, gather_around(): lax.ppermute(going_up, axis, [(d, (d + 1) % ways) for d in range(ways)])  189 us
    reduce_scatter x1, waiting for transfers between devices, local(): lax.psum_scatter(up_grad.astype(jnp.bfloat16), 'fsdp', scatter_dimension=...  147 us
    reduce_scatter x1, waiting for transfers between devices, local(): lax.psum_scatter(gate_grad.astype(jnp.bfloat16), 'fsdp', scatter_dimensio...  130 us
    all_gather x1, waiting for transfers between devices, local(): lax.all_gather(w_down, 'fsdp', axis=0, tiled=True)  95.2 us
    all_gather x1, waiting for transfers between devices, local(): lax.all_gather(w_up, 'fsdp', axis=0, tiled=True)  91.5 us
    dot_general x7, matrix products, dot_plain(): return jnp.dot(left, right, preferred_element_type=jnp.float32)  71.3 us
    reduce_scatter x1, waiting for transfers between devices, local(): lax.psum_scatter(value_grad.astype(jnp.bfloat16), 'fsdp', scatter_dimensi...  69.7 us
    reduce_scatter x1, waiting for transfers between devices, local(): mlp_sum = lax.psum_scatter(mlp_terms, 'tp', scatter_dimension=0, tiled=True)  69.7 us
  transfers between devices with their start and end apart: 29, of which 24 were waited for; matrix products, arithmetic and copies ran while one was open for 18% of the time, Pallas kernels for 0%

profile of v1, /device:TPU:0, one launch (start us, length us, event | category | flops | bytes accessed | tf_op | source)
XLA Modules:
  0.0 1896.3 jit_solution(4167739632740441464)
XLA Ops:
  13.2 48.7 %all-gather.14.cloned.1.call-done = bf16[2048,512]{1,0:T(8,128)(2,1)} async-done(((bf16[256,512]{1,0:T(8,128)(2,1)}), bf16[2048,512]{1,0:T(8,128)(2,1)}) %all-gather.14.cloned.1.call-update) | async-done | bytes 2097168 | tf_op jit(solution)/shard_map/all_gather | solution.py:109
  62.0 34.6 %all-gather.12.cloned.1.call-done = bf16[1024,2048]{1,0:T(8,128)(2,1)} async-done(((bf16[256,2048]{1,0:T(8,128)(2,1)}), bf16[1024,2048]{1,0:T(8,128)(2,1)}) %all-gather.12.cloned.1.call-update) | async-done | bytes 4194320 | tf_op jit(solution)/shard_map/all_gather | solution.py:107
  96.5 6.6 multiply_reduce_fusion.9
  103.1 44.7 %all-gather.16.cloned.1.call-done = bf16[2048,512]{1,0:T(8,128)(2,1)} async-done(((bf16[256,512]{1,0:T(8,128)(2,1)}), bf16[2048,512]{1,0:T(8,128)(2,1)}) %all-gather.16.cloned.1.call-update) | async-done | bytes 2097168 | tf_op jit(solution)/shard_map/all_gather | solution.py:110
  153.1 6.0 all-reduce.1
  180.3 17.2 all-gather.18.cloned.1.call-done
  204.0 6.1 fusion.60
  210.1 23.9 %while.42 = (s32[]{:T(128)}, bf16[2,512,4,128]{3,2,1,0:T(4,128)(2,1)}, f32[2,4,512]{2,1,0:T(4,128)S(1)}, s32[2]{0:T(128)S(1)}, s32[1,1024]{1,0:T(1,128)S(1)}, /*...) while((s32[]{:T(128)}, ...), condition=%wide.region_7.8_spmd.clone, body=%wide.region_4.7_spmd.clone.sunk | while | flops 1100741120 | bytes 35732304 | solution.py:165
  234.0 13.0 all-gather.20.cloned.1.call-done
  247.1 7.6 fusion.66
  255.5 69.2 %reduce-scatter.12.cloned.1.call-done = f32[256,2048]{1,0:T(8,128)} async-done(((f32[1024,2048]{1,0:T(8,128)}), f32[256,2048]{1,0:T(8,128)}) %reduce-scatter.12.cloned.1.call-update) | async-done | bytes 2097168 | tf_op jit(solution)/shard_map/reduce_scatter | solution.py:171
  334.3 52.7 %collective-permute-done = bf16[256,2048]{1,0:T(8,128)(2,1)S(1)} collective-permute-done((bf16[256,2048]{1,0:T(8,128)(2,1)S(1)}, bf16[256,2048]{1,0:T(8,128)(2,1)S(1)}, u32[]{:S(2)}, u32[]{:S(2)}) %collective-permute-start) | collective-permute-done | bytes 1048608 | tf_op jit(solution)/shard_map/ppermute | solution.py:19
  392.4 61.6 %collective-permute-done.2 = bf16[256,2048]{1,0:T(8,128)(2,1)} collective-permute-done((bf16[256,2048]{1,0:T(8,128)(2,1)S(1)}, bf16[256,2048]{1,0:T(8,128)(2,1)}, u32[]{:S(2)}, u32[]{:S(2)}) %collective-permute-start.2) | collective-permute-done | bytes 1048608 | tf_op jit(solution)/shard_map/ppermute | solution.py:19
  461.9 15.0 collective-permute-start.5
  478.0 45.0 %collective-permute-done.4 = bf16[256,2048]{1,0:T(8,128)(2,1)S(1)} collective-permute-done((bf16[256,2048]{1,0:T(8,128)(2,1)}, bf16[256,2048]{1,0:T(8,128)(2,1)S(1)}, u32[]{:S(2)}, u32[]{:S(2)}) %collective-permute-start.4) | collective-permute-done | bytes 1048608 | tf_op jit(solution)/shard_map/ppermute | solution.py:19
  535.6 29.6 %collective-permute-done.6 = bf16[256,2048]{1,0:T(8,128)(2,1)S(1)} collective-permute-done((bf16[256,2048]{1,0:T(8,128)(2,1)S(1)}, bf16[256,2048]{1,0:T(8,128)(2,1)S(1)}, u32[]{:S(2)}, u32[]{:S(2)}) %collective-permute-start.6) | collective-permute-done | bytes 1048608 | tf_op jit(solution)/shard_map/ppermute | solution.py:19
  566.3 34.2 %all-gather.22.cloned.1.call-done = bf16[1024,2048]{1,0:T(8,128)(2,1)} async-done(((bf16[256,2048]{1,0:T(8,128)(2,1)}), bf16[1024,2048]{1,0:T(8,128)(2,1)}) %all-gather.22.cloned.1.call-update) | async-done | bytes 4194320 | tf_op jit(solution)/shard_map/all_gather | solution.py:175
  600.5 13.4 fusion.81
  617.3 14.7 multiply_convert_fusion.3
  631.9 95.2 %all-gather.26.cloned.1.call-done = bf16[2048,2048]{1,0:T(8,128)(2,1)} async-done(((bf16[256,2048]{1,0:T(8,128)(2,1)}), bf16[2048,2048]{1,0:T(8,128)(2,1)}) %all-gather.26.cloned.1.call-update) | async-done | bytes 8388624 | tf_op jit(solution)/shard_map/all_gather | solution.py:115
  727.1 14.5 fusion.82
  741.7 69.7 %reduce-scatter.14.cloned.1.call-done = f32[256,2048]{1,0:T(8,128)} async-done(((f32[1024,2048]{1,0:T(8,128)}), f32[256,2048]{1,0:T(8,128)}) %reduce-scatter.14.cloned.1.call-update) | async-done | bytes 2097168 | tf_op jit(solution)/shard_map/reduce_scatter | solution.py:182
  817.1 34.0 %all-gather.28.cloned.1.call-done = bf16[1024,2048]{1,0:T(8,128)(2,1)} async-done(((bf16[256,2048]{1,0:T(8,128)(2,1)}), bf16[1024,2048]{1,0:T(8,128)(2,1)}) %all-gather.28.cloned.1.call-update) | async-done | bytes 4194320 | tf_op jit(solution)/shard_map/all_gather | solution.py:201
  851.1 19.8 %multiply_convert_fusion.1 = (bf16[1024,2048]{1,0:T(8,128)(2,1)}, bf16[1024,2048]{1,0:T(8,128)(2,1)S(1)}) fusion(f32[1024,2048]{1,0:T(8,128)} %copy-done.65, f32[1024,2048]{1,0:T(8,128)} %get-tuple-element.465, bf16[1024,2048]{1,0:T(8,128)(2,1)} %all-gather.28.cloned.1.call-done, bf16[2048,2048]{1,0:T(8,128)(2,1)} %all-gather.26.cloned.1.call-done), kind=kOutput, calls=%fused_computation.61 | convolution fusion | flops 8617197568 | bytes 37748736 | tf_op jit(solution)/shard_map/dot_general | solution.py:30
  872.9 13.2 fusion.83
  886.1 91.5 %all-gather.30.cloned.1.call-done = bf16[2048,2048]{1,0:T(8,128)(2,1)} async-done(((bf16[256,2048]{1,0:T(8,128)(2,1)}), bf16[2048,2048]{1,0:T(8,128)(2,1)}) %all-gather.30.cloned.1.call-update) | async-done | bytes 8388624 | tf_op jit(solution)/shard_map/all_gather | solution.py:192
  977.6 15.7 convolution_add_fusion
  993.5 69.5 %reduce-scatter.16.cloned.1.call-done = f32[256,2048]{1,0:T(8,128)} async-done(((f32[1024,2048]{1,0:T(8,128)}), f32[256,2048]{1,0:T(8,128)}) %reduce-scatter.16.cloned.1.call-update) | async-done | bytes 2097168 | tf_op jit(solution)/shard_map/reduce_scatter | solution.py:211
  1068.7 14.1 convolution_convert_fusion
  1082.9 14.0 convolution_convert_fusion.2
  1097.4 14.1 convolution_convert_fusion.1
  1120.5 6.3 convolution_convert_fusion.7
  1126.9 68.7 %while.43 = (s32[]{:T(128)}, f32[1024,4,128]{0,2,1:T(8,128)S(1)}, f32[1024,4,128]{0,2,1:T(8,128)}, f32[2,512,4,128]{3,1,2,0:T(8,128)}, s32[2]{0:T(128)S(1)}, /*i...) while((s32[]{:T(128)}, f32[1024,4,128]{0,2,1:T(8,128)S(1)}, ...), condition=%wide.region_17.18_spmd.clone, body=%wide.region_15.17_spmd.clone.sunk | while | flops 2720266752 | bytes 163650544 | solution.py:258
  1129.7 5.6 fusion.161
  1137.3 7.6 multiply_reduce_fusion.11
  1170.9 7.6 multiply_reduce_fusion.11
  1223.5 6.7 all-reduce
  1244.6 6.2 convolution_convert_fusion.3
  1252.7 5.9 fusion.50
  1265.3 6.1 add_convert_fusion
  1274.3 130.0 %reduce-scatter.28.cloned.1.call-done = bf16[256,2048]{1,0:T(8,128)(2,1)} async-done(((bf16[2048,2048]{1,0:T(8,128)(2,1)}), bf16[256,2048]{1,0:T(8,128)(2,1)}) %reduce-scatter.28.cloned.1.call-update) | async-done | bytes 1048592 | tf_op jit(solution)/shard_map/reduce_scatter | solution.py:310
  1407.1 147.3 %reduce-scatter.30.cloned.1.call-done = bf16[256,2048]{1,0:T(8,128)(2,1)} async-done(((bf16[2048,2048]{1,0:T(8,128)(2,1)}), bf16[256,2048]{1,0:T(8,128)(2,1)}) %reduce-scatter.30.cloned.1.call-update) | async-done | bytes 1048592 | tf_op jit(solution)/shard_map/reduce_scatter | solution.py:313
  1557.2 40.7 %psum.39 = f32[4,2048]{1,0:T(4,128)} all-reduce(f32[4,2048]{1,0:T(4,128)S(1)} %pad_maximum_fusion.2), channel_id=1, replica_groups=mesh['fsdp'=8,'tp'=4] {'fsdp','tp'}, use_global_device_ids=true, to_apply=%region_34.35 | all-reduce | flops 8192 | bytes 65536 | tf_op jit(solution)/shard_map/psum | solution.py:325
  1597.9 28.4 %reduce-scatter.22.cloned.1.call-done = bf16[256,512]{0,1:T(8,128)(2,1)} async-done(((bf16[2048,512]{0,1:T(8,128)(2,1)}), bf16[256,512]{0,1:T(8,128)(2,1)}) %reduce-scatter.22.cloned.1.call-update) | async-done | bytes 262160 | tf_op jit(solution)/shard_map/reduce_scatter | solution.py:301
  1628.2 69.7 %reduce-scatter.20.cloned.1.call-done = bf16[256,512]{0,1:T(8,128)(2,1)} async-done(((bf16[2048,512]{0,1:T(8,128)(2,1)}), bf16[256,512]{0,1:T(8,128)(2,1)}) %reduce-scatter.20.cloned.1.call-update) | async-done | bytes 262160 | tf_op jit(solution)/shard_map/reduce_scatter | solution.py:298
  1699.8 68.9 %reduce-scatter.26.cloned.1.call-done = bf16[256,512]{1,0:T(8,128)(2,1)} async-done(((bf16[2048,512]{1,0:T(8,128)(2,1)}), bf16[256,512]{1,0:T(8,128)(2,1)}) %reduce-scatter.26.cloned.1.call-update) | async-done | bytes 262160 | tf_op jit(solution)/shard_map/reduce_scatter | solution.py:307
  1770.5 69.7 %reduce-scatter.24.cloned.1.call-done = bf16[256,512]{0,1:T(8,128)(2,1)} async-done(((bf16[2048,512]{0,1:T(8,128)(2,1)}), bf16[256,512]{0,1:T(8,128)(2,1)}) %reduce-scatter.24.cloned.1.call-update) | async-done | bytes 262160 | tf_op jit(solution)/shard_map/reduce_scatter | solution.py:304
  1842.1 44.3 %reduce-scatter.18.cloned.1.call-done = bf16[256,2048]{1,0:T(8,128)(2,1)} async-done(((bf16[1024,2048]{1,0:T(8,128)(2,1)}), bf16[256,2048]{1,0:T(8,128)(2,1)}) %reduce-scatter.18.cloned.1.call-update) | async-done | bytes 1048592 | tf_op jit(solution)/shard_map/reduce_scatter | solution.py:290
  (334 shorter events, 234.4 us)
Async XLA Ops:
  7.2 54.8 %all-gather.14.cloned.1.call-start = ((), (), s32[]{:S(2)}) async-start(), calls=%async_computation.12 | async-start | bytes 2359296 | tf_op jit(solution)/shard_map/all_gather | solution.py:109
  7.9 88.6 %all-gather.12.cloned.1.call-start = ((), (), s32[]{:S(2)}) async-start(), calls=%async_computation.11 | async-start | bytes 5242880 | tf_op jit(solution)/shard_map/all_gather | solution.py:107
  8.7 139.1 %all-gather.16.cloned.1.call-start = ((), (), s32[]{:S(2)}) async-start(), calls=%async_computation.13 | async-start | bytes 2359296 | tf_op jit(solution)/shard_map/all_gather | solution.py:110
  9.4 188.0 %all-gather.18.cloned.1.call-start = ((), (), s32[]{:S(2)}) async-start(), calls=%async_computation.14 | async-start | bytes 2359296 | tf_op jit(solution)/shard_map/all_gather | solution.py:111
  10.0 237.1 %all-gather.20.cloned.1.call-start = ((), (), s32[]{:S(2)}) async-start(), calls=%async_computation.15 | async-start | bytes 2359296 | tf_op jit(solution)/shard_map/all_gather | solution.py:112
  10.6 314.2 %reduce-scatter.12.cloned.1.call-start = ((), (), s32[]{:S(2)}) async-start(), calls=%async_computation.16 | async-start | bytes 10485760 | tf_op jit(solution)/shard_map/reduce_scatter | solution.py:171
  10.8 148.3 %copy-start.53 = (f32[1,512]{1,0:T(1,128)}, f32[1,512]{1,0:T(1,128)S(1)}, u32[]{:S(2)}) copy-start(f32[1,512]{1,0:T(1,128)S(1)} %dynamic-slice.16) | copy-start | bytes 6148
  10.8 155.9 %copy-start.55 = (f32[1,512]{1,0:T(1,128)}, f32[1,512]{1,0:T(1,128)S(1)}, u32[]{:S(2)}) copy-start(f32[1,512]{1,0:T(1,128)S(1)} %constant_dynamic-slice_fusion.2) | copy-start | bytes 6148
  13.2 190.8 %copy-start.24 = (f32[1024,128]{1,0:T(8,128)}, f32[1024,128]{1,0:T(8,128)S(1)}, u32[]{:S(2)}) copy-start(f32[1024,128]{1,0:T(8,128)S(1)} %get-tuple-element.456) | copy-start | bytes 1572868
  13.2 190.8 %copy-start.29 = (f32[1024,128]{1,0:T(8,128)}, f32[1024,128]{1,0:T(8,128)S(1)}, u32[]{:S(2)}) copy-start(f32[1024,128]{1,0:T(8,128)S(1)} %get-tuple-element.457) | copy-start | bytes 1572868
  234.0 20.7 %copy-start.2 = (bf16[1,1024,4,128]{3,1,2,0:T(8,128)(2,1)}, bf16[1,1024,4,128]{3,1,2,0:T(8,128)(2,1)S(1)}, u32[]{:S(2)}) copy-start(bf16[1,1024,4,128]{3,1,2,0:T(8,128)(2,1)S(1)} %get-tuple-element.710) | copy-start | bytes 3145732
  234.0 20.7 %copy-start.6 = (bf16[1,1024,4,128]{3,1,2,0:T(8,128)(2,1)}, bf16[1,1024,4,128]{3,1,2,0:T(8,128)(2,1)S(1)}, u32[]{:S(2)}) copy-start(bf16[1,1024,4,128]{3,1,2,0:T(8,128)(2,1)S(1)} %get-tuple-element.711) | copy-start | bytes 3145732
  234.0 20.7 %copy-start.46 = (f32[2,4,512]{2,1,0:T(4,128)}, f32[2,4,512]{2,1,0:T(4,128)S(1)}, u32[]{:S(2)}) copy-start(f32[2,4,512]{2,1,0:T(4,128)S(1)} %get-tuple-element.258) | copy-start | bytes 49156
  254.7 72.1 %copy-start.27 = (bf16[256,2048]{1,0:T(8,128)(2,1)S(1)}, bf16[256,2048]{1,0:T(8,128)(2,1)}, u32[]{:S(2)}) copy-start(bf16[256,2048]{1,0:T(8,128)(2,1)} %param.15) | copy-start | bytes 3145732
  254.7 311.6 %all-gather.24.cloned.1.call-start = ((), (), s32[]{:S(2)}) async-start(), calls=%async_computation.18 | async-start | bytes 9437184 | tf_op jit(solution)/shard_map/all_gather | solution.py:113
  255.5 345.0 %all-gather.22.cloned.1.call-start = ((), (), s32[]{:S(2)}) async-start(), calls=%async_computation.17 | async-start | bytes 5242880 | tf_op jit(solution)/shard_map/all_gather | solution.py:175
  255.5 72.8 %copy-start.44 = (f32[1,2048]{1,0:T(1,128)}, f32[1,2048]{1,0:T(1,128)S(1)}, u32[]{:S(2)}) copy-start(f32[1,2048]{1,0:T(1,128)S(1)} %get-tuple-element.459) | copy-start | bytes 24580
  328.4 398.7 %all-gather.26.cloned.1.call-start = ((), (), s32[]{:S(2)}) async-start(), calls=%async_computation.19 | async-start | bytes 9437184 | tf_op jit(solution)/shard_map/all_gather | solution.py:115
  329.1 482.2 %reduce-scatter.14.cloned.1.call-start = ((), (), s32[]{:S(2)}) async-start(), calls=%async_computation.20 | async-start | bytes 10485760 | tf_op jit(solution)/shard_map/reduce_scatter | solution.py:182
  329.6 57.4 %collective-permute-start = (bf16[256,2048]{1,0:T(8,128)(2,1)S(1)}, bf16[256,2048]{1,0:T(8,128)(2,1)S(1)}, u32[]{:S(2)}, u32[]{:S(2)}) collective-permute-start(bf16[256,2048]{1,0:T(8,128)(2,1)S(1)} %copy-done.34), channel_id=1, source_target_pairs={{0,4},{4,8},{8,12},{12,16},{16,20},{20,24},{24,28},{28,0},{1,5},{5... | collective-permute-start | bytes 3145736 | tf_op jit(solution)/shard_map/ppermute | solution.py:19
  331.1 58.4 %collective-permute-start.1 = (bf16[256,2048]{1,0:T(8,128)(2,1)S(1)}, bf16[256,2048]{1,0:T(8,128)(2,1)S(1)}, u32[]{:S(2)}, u32[]{:S(2)}) collective-permute-start(bf16[256,2048]{1,0:T(8,128)(2,1)S(1)} %copy-done.34), channel_id=1, source_target_pairs={{0,28},{4,0},{8,4},{12,8},{16,12},{20,16},{24,20},{28,24},{1,29},{... | collective-permute-start | bytes 3145736 | tf_op jit(solution)/shard_map/ppermute | solution.py:22
  387.0 66.9 %collective-permute-start.2 = (bf16[256,2048]{1,0:T(8,128)(2,1)S(1)}, bf16[256,2048]{1,0:T(8,128)(2,1)}, u32[]{:S(2)}, u32[]{:S(2)}) collective-permute-start(bf16[256,2048]{1,0:T(8,128)(2,1)S(1)} %collective-permute-done), channel_id=1, source_target_pairs={{0,4},{4,8},{8,12},{12,16},{16,20},{20,24},{24,28},{28,0},{1,5},{5... | collective-permute-start | bytes 3145736 | tf_op jit(solution)/shard_map/ppermute | solution.py:19
  389.5 72.4 %collective-permute-start.3 = (bf16[256,2048]{1,0:T(8,128)(2,1)S(1)}, bf16[256,2048]{1,0:T(8,128)(2,1)}, u32[]{:S(2)}, u32[]{:S(2)}) collective-permute-start(bf16[256,2048]{1,0:T(8,128)(2,1)S(1)} %collective-permute-done.1), channel_id=1, source_target_pairs={{0,28},{4,0},{8,4},{12,8},{16,12},{20,16},{24,20},{28,24},{1,29},{... | collective-permute-start | bytes 3145736 | tf_op jit(solution)/shard_map/ppermute | solution.py:22
  453.9 69.0 %collective-permute-start.4 = (bf16[256,2048]{1,0:T(8,128)(2,1)}, bf16[256,2048]{1,0:T(8,128)(2,1)S(1)}, u32[]{:S(2)}, u32[]{:S(2)}) collective-permute-start(bf16[256,2048]{1,0:T(8,128)(2,1)} %collective-permute-done.2), channel_id=1, source_target_pairs={{0,4},{4,8},{8,12},{12,16},{16,20},{20,24},{24,28},{28,0},{1,5},{5... | collective-permute-start | bytes 3145736 | tf_op jit(solution)/shard_map/ppermute | solution.py:19
  460.9 16.0 copy-start.40
  461.9 72.6 %collective-permute-start.5 = (bf16[256,2048]{1,0:T(8,128)(2,1)}, bf16[256,2048]{1,0:T(8,128)(2,1)S(1)}, u32[]{:S(2)}, u32[]{:S(2)}) collective-permute-start(bf16[256,2048]{1,0:T(8,128)(2,1)} %collective-permute-done.3), channel_id=1, source_target_pairs={{0,28},{4,0},{8,4},{12,8},{16,12},{20,16},{24,20},{28,24},{1,29},{... | collective-permute-start | bytes 3145736 | tf_op jit(solution)/shard_map/ppermute | solution.py:22
  523.0 42.3 %collective-permute-start.6 = (bf16[256,2048]{1,0:T(8,128)(2,1)S(1)}, bf16[256,2048]{1,0:T(8,128)(2,1)S(1)}, u32[]{:S(2)}, u32[]{:S(2)}) collective-permute-start(bf16[256,2048]{1,0:T(8,128)(2,1)S(1)} %collective-permute-done.4), channel_id=1, source_target_pairs={{0,4},{4,8},{8,12},{12,16},{16,20},{20,24},{24,28},{28,0},{1,5},{5... | collective-permute-start | bytes 3145736 | tf_op jit(solution)/shard_map/ppermute | solution.py:19
  600.5 16.8 copy-start.63
  741.6 71.7 %copy-start.12 = (bf16[256,2048]{1,0:T(8,128)(2,1)S(1)}, bf16[256,2048]{1,0:T(8,128)(2,1)}, u32[]{:S(2)}) copy-start(bf16[256,2048]{1,0:T(8,128)(2,1)} %param.25) | copy-start | bytes 3145732
  741.6 109.4 %all-gather.28.cloned.1.call-start = ((), (), s32[]{:S(2)}) async-start(), calls=%async_computation.21 | async-start | bytes 5242880 | tf_op jit(solution)/shard_map/all_gather | solution.py:201
  816.4 161.1 %all-gather.30.cloned.1.call-start = ((), (), s32[]{:S(2)}) async-start(), calls=%async_computation.22 | async-start | bytes 9437184 | tf_op jit(solution)/shard_map/all_gather | solution.py:192
  817.0 246.0 %reduce-scatter.16.cloned.1.call-start = ((), (), s32[]{:S(2)}) async-start(), calls=%async_computation.23 | async-start | bytes 10485760 | tf_op jit(solution)/shard_map/reduce_scatter | solution.py:211
  993.2 69.8 %copy-start.9 = (f32[256,2048]{1,0:T(8,128)S(1)}, f32[256,2048]{1,0:T(8,128)}, u32[]{:S(2)}) copy-start(f32[256,2048]{1,0:T(8,128)} %reduce-scatter.12.cloned.1.call-done) | copy-start | bytes 6291460
  993.2 69.8 %copy-start.45 = (f32[1,2048]{1,0:T(1,128)S(1)}, f32[1,2048]{1,0:T(1,128)}, u32[]{:S(2)}) copy-start(f32[1,2048]{1,0:T(1,128)} %copy-done.44) | copy-start | bytes 24580
  993.2 69.8 %copy-start.60 = (f32[256]{0:T(256)S(1)}, f32[256]{0:T(256)}, u32[]{:S(2)}) copy-start(f32[256]{0:T(256)} %copy-done.59) | copy-start | bytes 3076
  993.3 127.2 %all-gather.32.cloned.1.call-start = ((), (), s32[]{:S(2)}) async-start(), calls=%async_computation.24 | async-start | bytes 5242880 | tf_op jit(solution)/shard_map/all_gather | solution.py:216
  1068.6 202.9 %reduce-scatter.32.cloned.1.call-start = ((), (), s32[]{:S(2)}) async-start(), calls=%async_computation.32 | async-start | bytes 9437184 | tf_op jit(solution)/shard_map/reduce_scatter | solution.py:316
  1082.8 321.5 %reduce-scatter.28.cloned.1.call-start = ((), (), s32[]{:S(2)}) async-start(), calls=%async_computation.30 | async-start | bytes 9437184 | tf_op jit(solution)/shard_map/reduce_scatter | solution.py:310
  1096.9 457.4 %reduce-scatter.30.cloned.1.call-start = ((), (), s32[]{:S(2)}) async-start(), calls=%async_computation.31 | async-start | bytes 9437184 | tf_op jit(solution)/shard_map/reduce_scatter | solution.py:313
  1111.5 514.8 %reduce-scatter.22.cloned.1.call-start = ((), (), s32[]{:S(2)}) async-start(), calls=%async_computation.27 | async-start | bytes 2359296 | tf_op jit(solution)/shard_map/reduce_scatter | solution.py:301
  1237.4 460.5 %reduce-scatter.20.cloned.1.call-start = ((), (), s32[]{:S(2)}) async-start(), calls=%async_computation.26 | async-start | bytes 2359296 | tf_op jit(solution)/shard_map/reduce_scatter | solution.py:298
  1244.3 524.3 %reduce-scatter.26.cloned.1.call-start = ((), (), s32[]{:S(2)}) async-start(), calls=%async_computation.29 | async-start | bytes 2359296 | tf_op jit(solution)/shard_map/reduce_scatter | solution.py:307
  1250.9 589.3 %reduce-scatter.24.cloned.1.call-start = ((), (), s32[]{:S(2)}) async-start(), calls=%async_computation.28 | async-start | bytes 2359296 | tf_op jit(solution)/shard_map/reduce_scatter | solution.py:304
  1258.7 627.7 %reduce-scatter.18.cloned.1.call-start = ((), (), s32[]{:S(2)}) async-start(), calls=%async_computation.25 | async-start | bytes 5242880 | tf_op jit(solution)/shard_map/reduce_scatter | solution.py:290
  1407.1 150.1 %copy-start.57 = (f32[2048]{0:T(1024)S(1)}, f32[2048]{0:T(1024)}, u32[]{:S(2)}) copy-start(f32[2048]{0:T(1024)} %get-tuple-element.387) | copy-start | bytes 24580
  1407.1 150.1 %copy-start.58 = (f32[2048]{0:T(1024)S(1)}, f32[2048]{0:T(1024)}, u32[]{:S(2)}) copy-start(f32[2048]{0:T(1024)} %get-tuple-element.381) | copy-start | bytes 24580
  1557.1 329.2 %copy-start.13 = (bf16[256,2048]{1,0:T(8,128)(2,1)S(1)}, bf16[256,2048]{1,0:T(8,128)(2,1)}, u32[]{:S(2)}) copy-start(bf16[256,2048]{1,0:T(8,128)(2,1)} %param.25) | copy-start | bytes 3145732
  1557.1 329.2 %copy-start.21 = (f32[256,2048]{1,0:T(8,128)S(1)}, f32[256,2048]{1,0:T(8,128)}, u32[]{:S(2)}) copy-start(f32[256,2048]{1,0:T(8,128)} %reduce-scatter.16.cloned.1.call-done) | copy-start | bytes 6291460
  (58 other events, 236.1 us)
Sparse Core Ops, SparseCore 0:
  10.1 51.7 all-gather.13
  63.5 32.9 all-gather.11
  98.7 49.0 all-gather.15
  149.8 47.6 all-gather.17
  199.4 47.6 all-gather.19
  254.8 69.9 reduce-scatter.11
  326.9 237.5 all-gather.23
  566.7 33.7 all-gather.21
  602.6 124.4 all-gather.25
  741.7 69.5 reduce-scatter.13
  816.6 34.4 all-gather.27
  853.0 124.4 all-gather.29
  993.4 69.5 reduce-scatter.15
  1068.7 34.4 all-gather.31
  1106.7 147.4 reduce-scatter.31
  1257.7 146.5 reduce-scatter.27
  1407.7 146.5 reduce-scatter.29
  1557.7 68.5 reduce-scatter.21
  1629.9 67.9 reduce-scatter.19
  1701.3 67.3 reduce-scatter.25
  1772.2 67.9 reduce-scatter.23
  1842.7 43.6 reduce-scatter.17
